TPU v7x, 32 devices: a whole 2x2x4 slice. The times are simulated.
32 devices in a mesh: ens: 4 (over y, x), slab: 8 (over z, core).
Axes of the slice: x: 2, y: 2, z: 4, core: 2. Of those that a mesh axis runs over, the one named last changes fastest.
Arguments:
- velocity: float32 [4, 3, 8, 2048, 1024], P('ens', None, None, 'slab'), may hold values from -6 to 6
- cutoffs: int32 [4, 2, 8], P('ens'), may hold values from 128 to 511, as said below
- plane_index: int32 [4], P('ens'), may hold values from 0 to 2047
- boundary_index: int32 [4], P('ens'), may hold values from 0 to 2047
Outputs:
- blended: float32 [4, 3, 8, 2048, 1024], P('ens', None, None, 'slab')
Inputs may be any that keep to these rules, and one draw needn't show every extreme that they name: `cutoffs`: row 0 lies in 256 to 511 and row 1 in 128 to 255; in every member some level has row 0 equal to 511 and some level has row 1 equal to 255.
All inputs are finite; a program needn't handle non-finite values.
Results may differ from a plain program's by a relative error of at most 0.0003.
Values sent between devices are 32-bit elements; how exact they have to be, the bound alone decides.
A program may use at most 128 MiB of HBM per device.

v0:
```python
import math

import jax
import jax.numpy as jnp
from jax import lax
from jax.sharding import PartitionSpec as P

KX = 512
KY = 256


highest = lax.Precision.HIGHEST


def spread(value, axis, source):
    kept = jnp.where(lax.axis_index(axis) == source, value, 0).astype(value.dtype)
    return lax.psum(kept, axis)


def shifted(block, axis, distance):
    devices = range(lax.axis_size(axis))
    route = [((i - distance) % len(devices), i) for i in devices]
    return lax.ppermute(block, axis, route)


def basis_pair(length, mode_count):
    position = jnp.arange(length, dtype=jnp.int32)
    wavenum = jnp.arange(mode_count, dtype=jnp.int32)
    angles = (position[:, None] * wavenum[None, :] % length).astype(jnp.float32) * (
        2.0 * math.pi / length
    )
    basis_cols = jnp.concatenate([jnp.cos(angles), jnp.sin(angles)], axis=1)
    weight = jnp.where(wavenum == 0, 1.0, 2.0).astype(jnp.float32) / length
    weight = jnp.concatenate([weight, weight])
    return (basis_cols * weight[None, :], basis_cols.T)


def mode_keep(levels_cut, mode_count):
    wavenum = jnp.tile(jnp.arange(mode_count, dtype=jnp.int32), 2)
    return (wavenum[None, :] <= levels_cut[:, None]).astype(jnp.float32)


def x_filter(columns, analysis_x, synthesis_x, keep_x):
    coeffs = (
        jnp.einsum("xk,czxj->czkj", analysis_x, columns, precision=highest)
        * keep_x[None, :, :, None]
    )
    return jnp.einsum("kx,czkj->czxj", synthesis_x, coeffs, precision=highest)


def on_device(velocity, cutoffs, plane_index, boundary_index):
    devices = lax.axis_size("slab")
    member_rows = velocity.shape[3]
    across = velocity.shape[4]
    along = member_rows * devices
    analysis_x, synthesis_x = basis_pair(along, KX)
    analysis_y, synthesis_y = basis_pair(across, KY)
    keep_x = mode_keep(cutoffs[0, 0], KX)
    keep_y = mode_keep(cutoffs[0, 1], KY)
    own_field = velocity[0]
    spectra = (
        jnp.einsum("czxy,yj->czxj", own_field, analysis_y, precision=highest)
        * keep_y[None, :, None, :]
    )
    columns = lax.all_to_all(spectra, "slab", split_axis=3, concat_axis=2, tiled=True)
    smooth = x_filter(columns, analysis_x, synthesis_x, keep_x)
    returned = lax.all_to_all(smooth, "slab", split_axis=2, concat_axis=3, tiled=True)
    result = jnp.einsum("czxj,jy->czxy", returned, synthesis_y, precision=highest)
    first_row = lax.axis_index("slab") * member_rows
    local_index = jnp.clip(plane_index[0] - first_row, 0, member_rows - 1)
    plane_part = lax.dynamic_index_in_dim(result, local_index, 2, keepdims=False)
    source_plane = spread(plane_part, "slab", plane_index[0] // member_rows)
    inflow = shifted(source_plane, "ens", 1)
    streamwise = first_row + jnp.arange(member_rows, dtype=jnp.int32)
    offset = jnp.abs(streamwise - boundary_index[0])
    distance = jnp.minimum(offset, along - offset)
    relax = jnp.exp(-distance.astype(jnp.float32) / (along / 4.0))
    weight = relax[None, None, :, None]
    blended = result + weight * (inflow[:, :, None, :] - result)
    return blended[None]


def solution(mesh):
    in_specs = (P("ens", None, None, "slab", None), P("ens", None, None), P("ens"), P("ens"))
    out_specs = P("ens", None, None, "slab", None)
    return jax.shard_map(
        on_device, mesh=mesh, in_specs=in_specs, out_specs=out_specs, check_vma=False
    )
```

profile of v0, /device:TPU:0, one launch (start us, length us, event | category | flops | bytes accessed | tf_op | source)
XLA Modules:
  0.0 1089.4 jit_solution(2496585179114449928)
XLA Ops:
  6.5 4.1 fusion.37
  10.7 0.8 slice_bitcast_fusion
  11.4 0.1 compare_convert_fusion.1
  11.5 84.5 %bitcast_multiply_fusion = f32[3,8,256,512]{2,3,1,0:T(8,128)} fusion(f32[8,512]{1,0:T(8,128)S(1)} %compare_convert_fusion.1, f32[1,3,8,256,1024]{4,3,2,1,0:T(8,128)} %param.4, f32[1024,256]{1,0:T(8,128)S(1)} %get-tuple-element.7, f32[1024,256]{1,0:T(8,128)S(1)} %get-tuple-element.8, f32[512]{0:T(512)S(1)} %pad_maximum_fusion.7), kind=kOutput, calls=%fused_computation.3 | convolution fusion | flops 38658899968 | bytes 39864320 | tf_op jit(solution)/shard_map/czxy,yj->czxj/dot_general | solution.py:62
  96.0 16.3 %copy.17 = f32[3,8,256,512]{2,1,0,3:T(8,128)} copy(f32[3,8,256,512]{2,3,1,0:T(8,128)} %bitcast_multiply_fusion) | data formatting | bytes 25165824 | tf_op jit(solution)/shard_map/mul | solution.py:62
  112.3 6.6 all-to-all-start
  119.0 0.1 compare_convert_fusion
  119.0 17.5 %fusion.27 = (f32[2048,512]{1,0:T(8,128)}, f32[2048,512]{1,0:T(8,128)}) fusion(), kind=kLoop, calls=%fused_computation.29 | loop fusion | flops 14680064 | bytes 8388608 | tf_op jit(solution)/shard_map/sin | solution.py:32
  136.6 256.1 %all-to-all-done = f32[3,8,256,512]{2,1,0,3:T(8,128)} async-done(((f32[3,8,256,512]{2,1,0,3:T(8,128)}), f32[3,8,256,512]{2,1,0,3:T(8,128)}, u32[]{:S(2)}, u32[]{:S(2)}) %all-to-all-start) | async-done | bytes 12582944 | tf_op jit(solution)/shard_map/all_to_all | solution.py:65
  392.7 16.6 %copy.36 = f32[3,8,256,8,64]{2,3,4,1,0:T(8,128)} copy(f32[3,8,256,8,64]{2,1,0,4,3:T(8,128)} %bitcast.4) | data formatting | bytes 25165824 | tf_op jit(solution)/shard_map/all_to_all | solution.py:65
  409.3 13.6 %all_to_all.29 = f32[3,8,2048,64]{2,3,1,0:T(8,128)} reshape(f32[3,8,8,256,64]{3,2,4,1,0:T(8,128)} %bitcast.77) | data formatting | bytes 25165824 | tf_op jit(solution)/shard_map/all_to_all | solution.py:65
  423.0 0.0 copy-start.1
  423.0 0.0 copy-start.2
  423.0 47.2 %fusion.4 = f32[3,8,64,1024]{3,2,1,0:T(8,128)} fusion(f32[3,8,2048,64]{2,3,1,0:T(8,128)} %all_to_all.29, f32[2048,512]{1,0:T(8,128)} %get-tuple-element.9, f32[2048,512]{1,0:T(8,128)} %get-tuple-element.10, f32[1024]{0:T(1024)S(1)} %pad_maximum_fusion.6), kind=kOutput, calls=%fused_computation.8 | convolution fusion | flops 38658899968 | bytes 27267072 | tf_op jit(solution)/shard_map/xk,czxj->czkj/dot_general | solution.py:45
  470.2 0.0 copy-done.1
  470.2 0.0 copy-done.2
  470.2 44.3 %fusion.9 = f32[3,8,2048,64]{2,3,1,0:T(8,128)} fusion(f32[2048,512]{1,0:T(8,128)S(1)} %copy-done.1, f32[2048,512]{1,0:T(8,128)S(1)} %copy-done.2, f32[3,8,64,1024]{3,2,1,0:T(8,128)} %fusion.4, f32[8,1024]{1,0:T(8,128)S(1)} %compare_convert_fusion), kind=kOutput, calls=%fused_computation.16 | convolution fusion | flops 38658375680 | bytes 27295744 | tf_op jit(solution)/shard_map/kx,czkj->czxj/dot_general | solution.py:48
  514.5 17.7 %copy.19 = f32[3,8,2048,64]{3,1,0,2:T(8,128)} copy(f32[3,8,2048,64]{2,3,1,0:T(8,128)} %fusion.9) | data formatting | bytes 25165824 | tf_op jit(solution)/shard_map/kx,czkj->czxj/transpose | solution.py:48
  532.2 20.5 %reshape.91 = f32[8,1,393216]{2,1,0:T(1,128)} reshape(f32[2048,3,8,64]{3,2,1,0:T(8,128)} %bitcast.74) | data formatting | bytes 25165824
  552.7 5.3 all-to-all-start.1
  558.1 0.0 all-reduce.2.cloned.1.call-start
  558.8 273.0 %all-to-all-done.1 = f32[8,1,393216]{2,1,0:T(1,128)} async-done(((f32[8,1,393216]{2,1,0:T(1,128)}), f32[8,1,393216]{2,1,0:T(1,128)}, u32[]{:S(2)}, u32[]{:S(2)}) %all-to-all-start.1) | async-done | bytes 12582944 | tf_op jit(solution)/shard_map/all_to_all | solution.py:67
  831.8 0.5 broadcast.88
  832.3 36.8 %reduce = f32[8,393216]{1,0:T(8,128)} reduce(f32[8,1,393216]{2,1,0:T(1,128)} %all-to-all-done.1, f32[]{:T(128)} %broadcast.88), dimensions={1}, to_apply=%all_to_all.30.reduce_sub_computation | reduce | bytes 25165828 | tf_op jit(solution)/shard_map/all_to_all | solution.py:67
  869.1 23.2 %reshape.92 = f32[2048,3,8,64]{3,2,1,0:T(8,128)} reshape(f32[8,393216]{1,0:T(8,128)} %reduce) | data formatting | bytes 25165824
  892.3 18.7 %copy.21 = f32[3,8,256,8,64]{2,4,3,1,0:T(8,128)} copy(f32[3,8,256,8,64]{4,1,0,2,3:T(8,128)} %bitcast.75) | data formatting | bytes 25165824 | tf_op jit(solution)/shard_map/all_to_all | solution.py:67
  911.0 85.2 %fusion.24 = f32[3,8,256,1024]{3,2,1,0:T(8,128)S(1)} fusion(f32[3,8,256,512]{2,3,1,0:T(8,128)} %bitcast.76, f32[1024,256]{1,0:T(8,128)S(1)} %get-tuple-element.7, f32[1024,256]{1,0:T(8,128)S(1)} %get-tuple-element.8), kind=kOutput, calls=%fused_computation.26 | convolution fusion | flops 38655229952 | bytes 39845888 | tf_op jit(solution)/shard_map/czxj,jy->czxy/dot_general | solution.py:68
  996.1 0.0 copy-start
  996.2 8.9 copy-done
  1005.1 0.1 broadcast_select_fusion
  1005.2 0.7 copy.37
  1005.8 0.0 all-reduce.2.cloned.1.call-update
  1006.5 51.2 %all-reduce.2.cloned.1.call-done = f32[3,8,1024]{2,1,0:T(8,128)} async-done(((f32[3,8,1024]{2,1,0:T(8,128)}), f32[3,8,1024]{2,1,0:T(8,128)}) %all-reduce.2.cloned.1.call-update) | async-done | bytes 98320 | tf_op jit(solution)/shard_map/psum | solution.py:17
  1057.7 1.5 collective-permute-start
  1059.2 4.2 collective-permute-done
  1063.4 18.8 %add_bitcast_fusion = f32[1,3,8,256,1024]{4,3,2,1,0:T(8,128)} fusion(f32[3,8,256,1024]{3,2,1,0:T(8,128)} %copy-done, f32[3,8,1024]{2,1,0:T(8,128)S(1)} %collective-permute-done, f32[256]{0:T(256)S(1)} %fusion.42), kind=kLoop, calls=%fused_computation.2 | loop fusion | flops 18874368 | bytes 50430976 | tf_op jit(solution)/shard_map/broadcast_in_dim | solution.py:80
  (9 shorter events, 0.1 us)
Async XLA Ops:
  112.3 280.4 %all-to-all-start = ((f32[3,8,256,512]{2,1,0,3:T(8,128)}), f32[3,8,256,512]{2,1,0,3:T(8,128)}, u32[]{:S(2)}, u32[]{:S(2)}) async-start(f32[3,8,256,512]{2,1,0,3:T(8,128)} %copy.17), calls=%async_computation | async-start | bytes 25165824 | tf_op jit(solution)/shard_map/all_to_all | solution.py:65
  423.0 47.2 %copy-start.1 = (f32[2048,512]{1,0:T(8,128)S(1)}, f32[2048,512]{1,0:T(8,128)}, u32[]{:S(2)}) copy-start(f32[2048,512]{1,0:T(8,128)} %get-tuple-element.9) | copy-start | bytes 12582916
  423.0 47.2 %copy-start.2 = (f32[2048,512]{1,0:T(8,128)S(1)}, f32[2048,512]{1,0:T(8,128)}, u32[]{:S(2)}) copy-start(f32[2048,512]{1,0:T(8,128)} %get-tuple-element.10) | copy-start | bytes 12582916
  552.7 279.1 %all-to-all-start.1 = ((f32[8,1,393216]{2,1,0:T(1,128)}), f32[8,1,393216]{2,1,0:T(1,128)}, u32[]{:S(2)}, u32[]{:S(2)}) async-start(f32[8,1,393216]{2,1,0:T(1,128)} %reshape.91), calls=%async_computation.1 | async-start | bytes 25165824 | tf_op jit(solution)/shard_map/all_to_all | solution.py:67
  558.1 499.6 %all-reduce.2.cloned.1.call-start = ((), (), s32[]{:S(2)}) async-start(), calls=%async_computation.2 | async-start | bytes 196608 | tf_op jit(solution)/shard_map/psum | solution.py:17
  996.1 8.9 copy-start
  1057.7 5.7 collective-permute-start
Sparse Core Ops, SparseCore 0:
  1006.0 51.6 all-reduce.1
where the time goes:
time: 1090 us
  waiting for transfers between devices  585 us (54%)
  matrix products  261 us (24%)
  local copies, waits for them, and re-layouts  138 us (13%)
  other arithmetic  77.5 us (7%)
  between operations  15.2 us (1%)
  starting transfers between devices  13.4 us (1%)
    all_to_all x1, waiting for transfers between devices, on_device(): lax.all_to_all(smooth, 'slab', split_axis=2, concat_axis=3, tiled=True)  273 us
    all_to_all x1, waiting for transfers between devices, on_device(): lax.all_to_all(spectra, 'slab', split_axis=3, concat_axis=2, tiled=True)  256 us
    dot_general x1, matrix products, on_device(): jnp.einsum('czxj,jy->czxy', returned, synthesis_y, precision=highest)  85.2 us
    dot_general x1, matrix products, on_device(): jnp.einsum('czxy,yj->czxj', own_field, analysis_y, precision=highest)  84.5 us
    unnamed x13, local copies, waits for them, and re-layouts  53.3 us
    psum x1, waiting for transfers between devices, spread(): return lax.psum(kept, axis)  51.2 us
    dot_general x1, matrix products, x_filter(): jnp.einsum('xk,czxj->czkj', analysis_x, columns, precision=highest)  47.2 us
    dot_general x1, matrix products, x_filter(): return jnp.einsum('kx,czkj->czxj', synthesis_x, coeffs, precision=highest)  44.3 us
  transfers between devices with their start and end apart: 4, of which 4 were waited for; matrix products, arithmetic and copies ran while one was open for 2% of the time, Pallas kernels for 0%

commit v1 on v0

v1 whole, which is shorter than its diff:
```python
import functools
import math

import jax
import jax.numpy as jnp
from jax import lax
from jax.experimental import pallas as pl
from jax.experimental.pallas import tpu as pltpu
from jax.sharding import PartitionSpec as P

KX = 512
KY = 256
CHUNK = 4

f32 = jnp.float32
bf16 = jnp.bfloat16

NN = (((1,), (0,)), ((), ()))
NT = (((1,), (1,)), ((), ()))


def halves(value):
    high = value.astype(bf16)
    return high, (value - high.astype(f32)).astype(bf16)


def table_halves(value):
    high = lax.reduce_precision(value, 8, 7)
    return high.astype(bf16), (value - high).astype(bf16)


def dot3(left, right, dims):
    (lh, ll), (rh, rl) = left, right
    dot = functools.partial(lax.dot_general, dimension_numbers=dims, preferred_element_type=f32)
    return dot(lh, rh) + (dot(ll, rh) + dot(lh, rl))


def analyse_y_kernel(field, bh, bl, out):
    devices, _, width, rows = out.shape
    coeffs = dot3((bh[...], bl[...]), halves(field[0]), NT)
    out[...] = coeffs.reshape(devices, 1, width, rows)


def analyse_x_kernel(lines, ch, cl, fx, fy, out):
    devices, planes, width, rows = lines.shape
    total = None
    for d in range(devices):
        part = dot3(
            halves(lines[d].reshape(planes * width, rows)),
            (ch[pl.ds(d * rows, rows), :], cl[pl.ds(d * rows, rows), :]),
            NN,
        )
        total = part if total is None else total + part
    out[...] = total.reshape(planes, width, -1) * fx[...] * fy[...]


def synthesise_x_kernel(spectra, ch, cl, relax, inflow, out):
    planes, width, modes = spectra.shape
    smooth = dot3(halves(spectra[...].reshape(planes * width, modes)), (ch[...], cl[...]), NT)
    smooth = smooth.reshape(planes, width, -1)
    out[0] = smooth + relax[0][None] * (inflow[...] - smooth)


def synthesise_y_kernel(coeffs, bh, bl, *refs):
    out = refs[-1]
    devices, _, width, rows = coeffs.shape
    lines = coeffs[...].reshape(devices * width, rows).T
    out[0] = dot3(halves(lines), (bh[...], bl[...]), NN)


def cost(flops, nbytes):
    return pl.CostEstimate(flops=int(flops), bytes_accessed=int(nbytes), transcendentals=0)


def params(n):
    return pltpu.CompilerParams(dimension_semantics=("arbitrary",) * n, vmem_limit_bytes=60 * 2**20)


def waves(wavenum, position, length):
    angles = (wavenum * position % length).astype(f32) * (2.0 * math.pi / length)
    return angles


def weights(mode_count, length):
    wavenum = jnp.arange(mode_count, dtype=jnp.int32)
    weight = jnp.where(wavenum == 0, 1.0, 2.0).astype(f32) / length
    return jnp.concatenate([weight, weight])


def on_device(velocity, cutoffs, plane_index, boundary_index):
    devices = lax.axis_size("slab")
    members = lax.axis_size("ens")
    me = lax.axis_index("slab")
    comps, levels, rows, across = velocity.shape[1:]
    along = rows * devices
    planes = comps * levels
    jtot, ktot = 2 * KY, 2 * KX
    width = jtot // devices
    size = CHUNK
    field = velocity.reshape(planes, rows, across)

    ky = jnp.arange(KY, dtype=jnp.int32)
    ang_y = waves(ky[:, None], jnp.arange(across, dtype=jnp.int32)[None, :], across)
    bh, bl = table_halves(jnp.concatenate([jnp.cos(ang_y), jnp.sin(ang_y)], axis=0))
    kx = jnp.arange(KX, dtype=jnp.int32)
    ang_x = waves(jnp.arange(along, dtype=jnp.int32)[:, None], kx[None, :], along)
    ch, cl = table_halves(jnp.concatenate([jnp.cos(ang_x), jnp.sin(ang_x)], axis=1))

    kx2 = jnp.tile(kx, 2)
    fx = (kx2[None, :] <= cutoffs[0, 0][:, None]).astype(f32) * weights(KX, along)[None]
    fx = jnp.tile(fx, (comps, 1))[:, None, :]
    fy = (jnp.tile(ky, 2)[None, :] <= cutoffs[0, 1][:, None]).astype(f32) * weights(KY, across)[None]
    fy = lax.dynamic_slice_in_dim(fy, me * width, width, 1)
    fy = jnp.tile(fy, (comps, 1))[:, :, None]

    ang_p = waves(plane_index[0], kx, along)
    at_plane = jnp.concatenate([jnp.cos(ang_p), jnp.sin(ang_p)])
    offset = jnp.abs(jnp.arange(along, dtype=jnp.int32) - boundary_index[0])
    distance = jnp.minimum(offset, along - offset)
    relax = jnp.exp(-distance.astype(f32) / (along / 4.0)).reshape(devices, 1, rows)

    kblock = 256
    route = [((i - 1) % members, i) for i in range(members)]
    sends = []
    for g in range(planes // size):
        first = g * size
        sends.append(
            pl.pallas_call(
                analyse_y_kernel,
                grid=(size,),
                in_specs=[
                    pl.BlockSpec((1, rows, across), lambda i, first=first: (first + i, 0, 0)),
                    pl.BlockSpec((jtot, across), lambda i: (0, 0)),
                    pl.BlockSpec((jtot, across), lambda i: (0, 0)),
                ],
                out_specs=pl.BlockSpec((devices, 1, width, rows), lambda i: (0, i, 0, 0)),
                out_shape=jax.ShapeDtypeStruct((devices, size, width, rows), f32),
                cost_estimate=cost(6 * size * rows * across * jtot, 6 * size * rows * across),
                compiler_params=params(1),
                name="analyse_y",
            )(field, bh, bl)
        )
    lines = [lax.all_to_all(s, "slab", 0, 0, tiled=True) for s in sends]

    backs = []
    for g, got in enumerate(lines):
        first = g * size
        spectra = pl.pallas_call(
            analyse_x_kernel,
            grid=(ktot // kblock,),
            in_specs=[
                pl.BlockSpec((devices, size, width, rows), lambda k: (0, 0, 0, 0)),
                pl.BlockSpec((along, kblock), lambda k: (0, k)),
                pl.BlockSpec((along, kblock), lambda k: (0, k)),
                pl.BlockSpec((size, 1, kblock), lambda k: (0, 0, k)),
                pl.BlockSpec((size, width, 1), lambda k: (0, 0, 0)),
            ],
            out_specs=pl.BlockSpec((size, width, kblock), lambda k: (0, 0, k)),
            out_shape=jax.ShapeDtypeStruct((size, width, ktot), f32),
            cost_estimate=cost(6 * size * width * along * ktot, 4 * size * width * along + 4 * along * ktot),
            compiler_params=params(1),
            name="analyse_x",
        )(got, ch, cl, fx[first : first + size], fy[first : first + size])
        handed = jnp.sum(spectra * at_plane, axis=-1)
        inflow = lax.ppermute(handed, "ens", route)[:, :, None]
        smooth = pl.pallas_call(
            synthesise_x_kernel,
            grid=(devices,),
            in_specs=[
                pl.BlockSpec((size, width, ktot), lambda d: (0, 0, 0)),
                pl.BlockSpec((rows, ktot), lambda d: (d, 0)),
                pl.BlockSpec((rows, ktot), lambda d: (d, 0)),
                pl.BlockSpec((1, 1, rows), lambda d: (d, 0, 0)),
                pl.BlockSpec((size, width, 1), lambda d: (0, 0, 0)),
            ],
            out_specs=pl.BlockSpec((1, size, width, rows), lambda d: (d, 0, 0, 0)),
            out_shape=jax.ShapeDtypeStruct((devices, size, width, rows), f32),
            cost_estimate=cost(6 * size * width * along * ktot, 4 * size * width * along + 4 * along * ktot),
            compiler_params=params(1),
            name="synthesise_x",
        )(spectra, ch, cl, relax, inflow)
        backs.append(lax.all_to_all(smooth, "slab", 0, 0, tiled=True))

    result = None
    for g, back in enumerate(backs):
        first = g * size
        extra = [] if result is None else [result]
        result = pl.pallas_call(
            synthesise_y_kernel,
            grid=(size,),
            in_specs=[
                pl.BlockSpec((devices, 1, width, rows), lambda i: (0, i, 0, 0)),
                pl.BlockSpec((jtot, across), lambda i: (0, 0)),
                pl.BlockSpec((jtot, across), lambda i: (0, 0)),
            ]
            + [pl.BlockSpec(memory_space=pl.ANY)] * len(extra),
            out_specs=pl.BlockSpec((1, rows, across), lambda i, first=first: (first + i, 0, 0)),
            out_shape=jax.ShapeDtypeStruct((planes, rows, across), f32),
            input_output_aliases={3: 0} if extra else {},
            cost_estimate=cost(6 * size * rows * across * jtot, 6 * size * rows * across),
            compiler_params=params(1),
            name="synthesise_y",
        )(back, bh, bl, *extra)
    return result.reshape(velocity.shape)


def solution(mesh):
    in_specs = (P("ens", None, None, "slab", None), P("ens", None, None), P("ens"), P("ens"))
    out_specs = P("ens", None, None, "slab", None)
    return jax.shard_map(
        on_device, mesh=mesh, in_specs=in_specs, out_specs=out_specs, check_vma=False
    )
```

time: 1090 us -> 716 us (0.66)
  matrix products: 261 us -> 0 us
  Pallas kernels: 0 us -> 196 us
  waiting for transfers between devices: 585 us -> 410 us
  local copies, waits for them, and re-layouts: 138 us -> 11 us
  other arithmetic: 77.5 us -> 29.6 us
  starting transfers between devices: 13.4 us -> 57.1 us
  between operations: 15.2 us -> 1.97 us
    dot_general x4 -> x0, matrix products: 261 us -> none  [the longest x1 85.2 us: on_device(): jnp.einsum('czxj,jy->czxy', returned, synthesis_y, precision=highest)]
    pallas_call x0 -> x24, Pallas kernels: none -> 196 us  [the longest x6 58.5 us: on_device(): pl.pallas_call(synthesise_x_kernel, grid=(devices,), in_specs=[pl.BlockSp...]
    all_to_all x2 -> x12, waiting for transfers between devices: 529 us -> 388 us  [the longest x6 206 us: on_device(): lines = [lax.all_to_all(s, 'slab', 0, 0, tiled=True) for s in sends]]
    psum x1 -> x0, waiting for transfers between devices: 51.2 us -> none  [spread(): return lax.psum(kept, axis)]
    all_to_all x4 -> x0, local copies, waits for them, and re-layouts: 49.4 us -> none  [the longest x2 30.3 us: on_device(): lax.all_to_all(spectra, 'slab', split_axis=3, concat_axis=2, tiled=True)]
    unnamed x13 -> x29, local copies, waits for them, and re-layouts: 53.3 us -> 3.95 us
    all_to_all x2 -> x12, starting transfers between devices: 11.9 us -> 52.4 us  [the longest x6 26.8 us: on_device(): lines = [lax.all_to_all(s, 'slab', 0, 0, tiled=True) for s in sends]]
    all_to_all x1 -> x0, other arithmetic: 36.8 us -> none  [on_device(): lax.all_to_all(smooth, 'slab', split_axis=2, concat_axis=3, tiled=True)]
  transfers between devices with their start and end apart: 4 -> 18, of which waited for: 4 -> 17; matrix products, arithmetic and copies ran while one was open for 2% -> 4% of each run, Pallas kernels for 0% -> 23%
where the time goes in v1:
time: 716 us; the launch traced here: 706 us
  waiting for transfers between devices  410 us (57%)
  Pallas kernels  196 us (27%)
  starting transfers between devices  57.1 us (8%)
  other arithmetic  29.6 us (4%)
  local copies, waits for them, and re-layouts  11 us (2%)
    all_to_all x6, waiting for transfers between devices, on_device(): lines = [lax.all_to_all(s, 'slab', 0, 0, tiled=True) for s in sends]  206 us
    all_to_all x6, waiting for transfers between devices, on_device(): backs.append(lax.all_to_all(smooth, 'slab', 0, 0, tiled=True))  182 us
    pallas_call x6, Pallas kernels, on_device(): pl.pallas_call(synthesise_x_kernel, grid=(devices,), in_specs=[pl.BlockSp...  58.5 us
    pallas_call x6, Pallas kernels, on_device(): pl.pallas_call(analyse_x_kernel, grid=(ktot // kblock,), in_specs=[pl.Blo...  49.6 us
    pallas_call x6, Pallas kernels, on_device(): pl.pallas_call(analyse_y_kernel, grid=(size,), in_specs=[pl.BlockSpec((1,...  43.9 us
    pallas_call x6, Pallas kernels, on_device(): pl.pallas_call(synthesise_y_kernel, grid=(size,), in_specs=[pl.BlockSpec(...  43.5 us
    all_to_all x6, starting transfers between devices, on_device(): lines = [lax.all_to_all(s, 'slab', 0, 0, tiled=True) for s in sends]  26.8 us
    all_to_all x6, starting transfers between devices, on_device(): backs.append(lax.all_to_all(smooth, 'slab', 0, 0, tiled=True))  25.6 us
  transfers between devices with their start and end apart: 18, of which 17 were waited for; matrix products, arithmetic and copies ran while one was open for 4% of the time, Pallas kernels for 23%

profile of v1, /device:TPU:0, one launch (start us, length us, event | category | flops | bytes accessed | tf_op | source)
XLA Modules:
  0.0 705.5 jit_solution(14727954610562285774)
XLA Ops:
  0.0 4.1 fusion.16
  5.8 7.3 %analyse_y.11 = f32[8,4,64,256]{3,2,1,0:T(8,128)} custom-call(f32[24,256,1024]{2,1,0:T(8,128)} %bitcast.30, bf16[512,1024]{1,0:T(8,128)(2,1)} %get-tuple-element.14.bh, bf16[512,1024]{1,0:T(8,128)(2,1)} %get-tuple-element.13.bl), custom_call_target="tpu_custom_call" | custom-call | flops 3221225472 | bytes 6291456 | tf_op jit(solution)/shard_map/analyse_y/pallas_call | solution.py:128
  13.1 6.4 all-to-all-start.10
  19.5 7.3 %analyse_y.10 = f32[8,4,64,256]{3,2,1,0:T(8,128)} custom-call(f32[24,256,1024]{2,1,0:T(8,128)} %bitcast.31, bf16[512,1024]{1,0:T(8,128)(2,1)} %get-tuple-element.14.bh, bf16[512,1024]{1,0:T(8,128)(2,1)} %get-tuple-element.13.bl), custom_call_target="tpu_custom_call" | custom-call | flops 3221225472 | bytes 6291456 | tf_op jit(solution)/shard_map/analyse_y/pallas_call | solution.py:128
  26.8 41.7 %all-to-all-done.10.lines = f32[8,4,64,256]{3,2,1,0:T(8,128)S(1)} async-done(((f32[8,4,64,256]{3,2,1,0:T(8,128)}), f32[8,4,64,256]{3,2,1,0:T(8,128)S(1)}, u32[]{:S(2)}, u32[]{:S(2)}) %all-to-all-start.10) | async-done | bytes 2097184 | tf_op jit(solution)/shard_map/all_to_all | solution.py:143
  68.5 4.4 all-to-all-start.8
  72.9 7.3 %analyse_y.9 = f32[8,4,64,256]{3,2,1,0:T(8,128)} custom-call(f32[24,256,1024]{2,1,0:T(8,128)} %bitcast.32, bf16[512,1024]{1,0:T(8,128)(2,1)} %get-tuple-element.14.bh, bf16[512,1024]{1,0:T(8,128)(2,1)} %get-tuple-element.13.bl), custom_call_target="tpu_custom_call" | custom-call | flops 3221225472 | bytes 6291456 | tf_op jit(solution)/shard_map/analyse_y/pallas_call | solution.py:128
  80.2 41.7 %all-to-all-done.8.lines = f32[8,4,64,256]{3,2,1,0:T(8,128)} async-done(((f32[8,4,64,256]{3,2,1,0:T(8,128)}), f32[8,4,64,256]{3,2,1,0:T(8,128)}, u32[]{:S(2)}, u32[]{:S(2)}) %all-to-all-start.8) | async-done | bytes 2097184 | tf_op jit(solution)/shard_map/all_to_all | solution.py:143
  125.5 7.3 %analyse_y.8 = f32[8,4,64,256]{3,2,1,0:T(8,128)} custom-call(f32[24,256,1024]{2,1,0:T(8,128)} %bitcast.33, bf16[512,1024]{1,0:T(8,128)(2,1)} %get-tuple-element.14.bh, bf16[512,1024]{1,0:T(8,128)(2,1)} %get-tuple-element.13.bl), custom_call_target="tpu_custom_call" | custom-call | flops 3221225472 | bytes 6291456 | tf_op jit(solution)/shard_map/analyse_y/pallas_call | solution.py:128
  132.9 41.6 %all-to-all-done.6.lines = f32[8,4,64,256]{3,2,1,0:T(8,128)S(1)} async-done(((f32[8,4,64,256]{3,2,1,0:T(8,128)}), f32[8,4,64,256]{3,2,1,0:T(8,128)S(1)}, u32[]{:S(2)}, u32[]{:S(2)}) %all-to-all-start.6) | async-done | bytes 2097184 | tf_op jit(solution)/shard_map/all_to_all | solution.py:143
  174.5 4.4 all-to-all-start.4
  178.9 7.3 %analyse_y.7 = f32[8,4,64,256]{3,2,1,0:T(8,128)} custom-call(f32[24,256,1024]{2,1,0:T(8,128)} %bitcast.34, bf16[512,1024]{1,0:T(8,128)(2,1)} %get-tuple-element.14.bh, bf16[512,1024]{1,0:T(8,128)(2,1)} %get-tuple-element.13.bl), custom_call_target="tpu_custom_call" | custom-call | flops 3221225472 | bytes 6291456 | tf_op jit(solution)/shard_map/analyse_y/pallas_call | solution.py:128
  186.2 41.7 %all-to-all-done.4.lines = f32[8,4,64,256]{3,2,1,0:T(8,128)} async-done(((f32[8,4,64,256]{3,2,1,0:T(8,128)}), f32[8,4,64,256]{3,2,1,0:T(8,128)}, u32[]{:S(2)}, u32[]{:S(2)}) %all-to-all-start.4) | async-done | bytes 2097184 | tf_op jit(solution)/shard_map/all_to_all | solution.py:143
  233.9 7.4 %analyse_y.6 = f32[8,4,64,256]{3,2,1,0:T(8,128)} custom-call(f32[24,256,1024]{2,1,0:T(8,128)} %bitcast.35, bf16[512,1024]{1,0:T(8,128)(2,1)} %get-tuple-element.14.bh, bf16[512,1024]{1,0:T(8,128)(2,1)} %get-tuple-element.13.bl), custom_call_target="tpu_custom_call" | custom-call | flops 3221225472 | bytes 6291456 | tf_op jit(solution)/shard_map/analyse_y/pallas_call | solution.py:128
  241.3 39.2 %all-to-all-done.2.lines = f32[8,4,64,256]{3,2,1,0:T(8,128)S(1)} async-done(((f32[8,4,64,256]{3,2,1,0:T(8,128)}), f32[8,4,64,256]{3,2,1,0:T(8,128)S(1)}, u32[]{:S(2)}, u32[]{:S(2)}) %all-to-all-start.2) | async-done | bytes 2097184 | tf_op jit(solution)/shard_map/all_to_all | solution.py:143
  280.5 4.5 all-to-all-start
  290.5 16.3 %fusion.8 = (f32[2048,512]{1,0:T(8,128)S(1)}, f32[2048,512]{1,0:T(8,128)S(1)}) fusion(), kind=kLoop, calls=%fused_computation.17 | loop fusion | flops 14680064 | bytes 8388608 | tf_op jit(solution)/shard_map/sin | solution.py:107
  306.8 4.2 fusion
  311.1 8.2 %analyse_x.11.spectra = f32[4,64,1024]{2,1,0:T(8,128)} custom-call(f32[8,4,64,256]{3,2,1,0:T(8,128)} %copy-done.3, bf16[2048,1024]{1,0:T(8,128)(2,1)} %get-tuple-element.12.ch, bf16[2048,1024]{1,0:T(8,128)(2,1)} %get-tuple-element.11.cl, f32[4,1,1024]{2,1,0:T(1,128)} %get-tuple-element.16.fx, f32[4,64,1]{2,1,0:T(8,128)} %copy.26.fy), custom_call_target="tpu_custom_call" | custom-call | flops 3221225472 | bytes 10485760 | tf_op jit(solution)/shard_map/analyse_x/pallas_call | solution.py:148
  319.3 8.3 %analyse_x.10.spectra = f32[4,64,1024]{2,1,0:T(8,128)} custom-call(f32[8,4,64,256]{3,2,1,0:T(8,128)} %all-to-all-done.8.lines, bf16[2048,1024]{1,0:T(8,128)(2,1)} %get-tuple-element.12.ch, bf16[2048,1024]{1,0:T(8,128)(2,1)} %get-tuple-element.11.cl, f32[4,1,1024]{2,1,0:T(1,128)} %get-tuple-element.15.fx, f32[4,64,1]{2,1,0:T(8,128)} %copy.25.fy), custom_call_target="tpu_custom_call" | custom-call | flops 3221225472 | bytes 10485760 | tf_op jit(solution)/shard_map/analyse_x/pallas_call | solution.py:148
  327.5 8.4 %analyse_x.9.spectra = f32[4,64,1024]{2,1,0:T(8,128)} custom-call(f32[8,4,64,256]{3,2,1,0:T(8,128)} %copy-done.4, bf16[2048,1024]{1,0:T(8,128)(2,1)} %get-tuple-element.12.ch, bf16[2048,1024]{1,0:T(8,128)(2,1)} %get-tuple-element.11.cl, f32[4,1,1024]{2,1,0:T(1,128)} %get-tuple-element.17.fx, f32[4,64,1]{2,1,0:T(8,128)} %copy.24.fy), custom_call_target="tpu_custom_call" | custom-call | flops 3221225472 | bytes 10485760 | tf_op jit(solution)/shard_map/analyse_x/pallas_call | solution.py:148
  336.0 8.2 %analyse_x.8.spectra = f32[4,64,1024]{2,1,0:T(8,128)} custom-call(f32[8,4,64,256]{3,2,1,0:T(8,128)} %all-to-all-done.4.lines, bf16[2048,1024]{1,0:T(8,128)(2,1)} %get-tuple-element.12.ch, bf16[2048,1024]{1,0:T(8,128)(2,1)} %get-tuple-element.11.cl, f32[4,1,1024]{2,1,0:T(1,128)} %get-tuple-element.18.fx, f32[4,64,1]{2,1,0:T(8,128)} %copy.23.fy), custom_call_target="tpu_custom_call" | custom-call | flops 3221225472 | bytes 10485760 | tf_op jit(solution)/shard_map/analyse_x/pallas_call | solution.py:148
  344.2 8.2 %analyse_x.7.spectra = f32[4,64,1024]{2,1,0:T(8,128)} custom-call(f32[8,4,64,256]{3,2,1,0:T(8,128)} %copy-done.5, bf16[2048,1024]{1,0:T(8,128)(2,1)} %get-tuple-element.12.ch, bf16[2048,1024]{1,0:T(8,128)(2,1)} %get-tuple-element.11.cl, f32[4,1,1024]{2,1,0:T(1,128)} %get-tuple-element.19.fx, f32[4,64,1]{2,1,0:T(8,128)} %copy.22.fy), custom_call_target="tpu_custom_call" | custom-call | flops 3221225472 | bytes 10485760 | tf_op jit(solution)/shard_map/analyse_x/pallas_call | solution.py:148
  352.4 8.3 %analyse_x.6.spectra = f32[4,64,1024]{2,1,0:T(8,128)} custom-call(f32[8,4,64,256]{3,2,1,0:T(8,128)} %all-to-all-done.lines, bf16[2048,1024]{1,0:T(8,128)(2,1)} %get-tuple-element.12.ch, bf16[2048,1024]{1,0:T(8,128)(2,1)} %get-tuple-element.11.cl, f32[4,1,1024]{2,1,0:T(1,128)} %slice.50.fx, f32[4,64,1]{2,1,0:T(8,128)} %copy.10.fy), custom_call_target="tpu_custom_call" | custom-call | flops 3221225472 | bytes 10485760 | tf_op jit(solution)/shard_map/analyse_x/pallas_call | solution.py:148
  368.4 9.7 %synthesise_x.11 = f32[8,4,64,256]{3,2,1,0:T(8,128)} custom-call(f32[4,64,1024]{2,1,0:T(8,128)} %analyse_x.11.spectra, bf16[2048,1024]{1,0:T(8,128)(2,1)} %get-tuple-element.12.ch, bf16[2048,1024]{1,0:T(8,128)(2,1)} %get-tuple-element.11.cl, f32[8,1,256]{2,1,0:T(1,128)} %fusion.21.relax, f32[4,64,1]{2,1,0:T(8,128)} %copy.21.inflow), custom_call_target="tpu_custom_call" | custom-call | flops 3221225472 | bytes 10485760 | tf_op jit(solution)/shard_map/synthesise_x/pallas_call | solution.py:166
  378.1 5.1 all-to-all-start.11
  388.5 9.8 %synthesise_x.7 = f32[8,4,64,256]{3,2,1,0:T(8,128)} custom-call(f32[4,64,1024]{2,1,0:T(8,128)} %analyse_x.7.spectra, bf16[2048,1024]{1,0:T(8,128)(2,1)} %get-tuple-element.12.ch, bf16[2048,1024]{1,0:T(8,128)(2,1)} %get-tuple-element.11.cl, f32[8,1,256]{2,1,0:T(1,128)} %fusion.21.relax, f32[4,64,1]{2,1,0:T(8,128)} %copy.13.inflow), custom_call_target="tpu_custom_call" | custom-call | flops 3221225472 | bytes 10485760 | tf_op jit(solution)/shard_map/synthesise_x/pallas_call | solution.py:166
  398.2 34.0 %all-to-all-done.11.coeffs = f32[8,4,64,256]{3,2,1,0:T(8,128)S(1)} async-done(((f32[8,4,64,256]{3,2,1,0:T(8,128)}), f32[8,4,64,256]{3,2,1,0:T(8,128)S(1)}, u32[]{:S(2)}, u32[]{:S(2)}) %all-to-all-start.11) | async-done | bytes 2097184 | tf_op jit(solution)/shard_map/all_to_all | solution.py:182
  432.2 4.4 all-to-all-start.3
  441.9 9.8 %synthesise_x.8 = f32[8,4,64,256]{3,2,1,0:T(8,128)} custom-call(f32[4,64,1024]{2,1,0:T(8,128)} %analyse_x.8.spectra, bf16[2048,1024]{1,0:T(8,128)(2,1)} %get-tuple-element.12.ch, bf16[2048,1024]{1,0:T(8,128)(2,1)} %get-tuple-element.11.cl, f32[8,1,256]{2,1,0:T(1,128)} %fusion.21.relax, f32[4,64,1]{2,1,0:T(8,128)} %copy.15.inflow), custom_call_target="tpu_custom_call" | custom-call | flops 3221225472 | bytes 10485760 | tf_op jit(solution)/shard_map/synthesise_x/pallas_call | solution.py:166
  451.7 34.0 %all-to-all-done.3.coeffs = f32[8,4,64,256]{3,2,1,0:T(8,128)} async-done(((f32[8,4,64,256]{3,2,1,0:T(8,128)}), f32[8,4,64,256]{3,2,1,0:T(8,128)}, u32[]{:S(2)}, u32[]{:S(2)}) %all-to-all-start.3) | async-done | bytes 2097184 | tf_op jit(solution)/shard_map/all_to_all | solution.py:182
  489.9 3.9 collective-permute-done.3
  494.6 9.8 %synthesise_x.9 = f32[8,4,64,256]{3,2,1,0:T(8,128)} custom-call(f32[4,64,1024]{2,1,0:T(8,128)} %analyse_x.9.spectra, bf16[2048,1024]{1,0:T(8,128)(2,1)} %get-tuple-element.12.ch, bf16[2048,1024]{1,0:T(8,128)(2,1)} %get-tuple-element.11.cl, f32[8,1,256]{2,1,0:T(1,128)} %fusion.21.relax, f32[4,64,1]{2,1,0:T(8,128)} %copy.17.inflow), custom_call_target="tpu_custom_call" | custom-call | flops 3221225472 | bytes 10485760 | tf_op jit(solution)/shard_map/synthesise_x/pallas_call | solution.py:166
  504.3 33.9 %all-to-all-done.5.coeffs = f32[8,4,64,256]{3,2,1,0:T(8,128)S(1)} async-done(((f32[8,4,64,256]{3,2,1,0:T(8,128)}), f32[8,4,64,256]{3,2,1,0:T(8,128)S(1)}, u32[]{:S(2)}, u32[]{:S(2)}) %all-to-all-start.5) | async-done | bytes 2097184 | tf_op jit(solution)/shard_map/all_to_all | solution.py:182
  538.2 4.4 all-to-all-start.7
  543.2 3.9 collective-permute-done.4
  547.9 9.7 %synthesise_x.10 = f32[8,4,64,256]{3,2,1,0:T(8,128)} custom-call(f32[4,64,1024]{2,1,0:T(8,128)} %analyse_x.10.spectra, bf16[2048,1024]{1,0:T(8,128)(2,1)} %get-tuple-element.12.ch, bf16[2048,1024]{1,0:T(8,128)(2,1)} %get-tuple-element.11.cl, f32[8,1,256]{2,1,0:T(1,128)} %fusion.21.relax, f32[4,64,1]{2,1,0:T(8,128)} %copy.19.inflow), custom_call_target="tpu_custom_call" | custom-call | flops 3221225472 | bytes 10485760 | tf_op jit(solution)/shard_map/synthesise_x/pallas_call | solution.py:166
  557.6 34.0 %all-to-all-done.7.coeffs = f32[8,4,64,256]{3,2,1,0:T(8,128)} async-done(((f32[8,4,64,256]{3,2,1,0:T(8,128)}), f32[8,4,64,256]{3,2,1,0:T(8,128)}, u32[]{:S(2)}, u32[]{:S(2)}) %all-to-all-start.7) | async-done | bytes 2097184 | tf_op jit(solution)/shard_map/all_to_all | solution.py:182
  600.6 9.8 %synthesise_x.6 = f32[8,4,64,256]{3,2,1,0:T(8,128)} custom-call(f32[4,64,1024]{2,1,0:T(8,128)} %analyse_x.6.spectra, bf16[2048,1024]{1,0:T(8,128)(2,1)} %get-tuple-element.12.ch, bf16[2048,1024]{1,0:T(8,128)(2,1)} %get-tuple-element.11.cl, f32[8,1,256]{2,1,0:T(1,128)} %fusion.21.relax, f32[4,64,1]{2,1,0:T(8,128)} %copy.11.inflow), custom_call_target="tpu_custom_call" | custom-call | flops 3221225472 | bytes 10485760 | tf_op jit(solution)/shard_map/synthesise_x/pallas_call | solution.py:166
  610.3 33.9 %all-to-all-done.9.coeffs = f32[8,4,64,256]{3,2,1,0:T(8,128)S(1)} async-done(((f32[8,4,64,256]{3,2,1,0:T(8,128)}), f32[8,4,64,256]{3,2,1,0:T(8,128)S(1)}, u32[]{:S(2)}, u32[]{:S(2)}) %all-to-all-start.9) | async-done | bytes 2097184 | tf_op jit(solution)/shard_map/all_to_all | solution.py:182
  644.2 4.6 all-to-all-start.1
  648.8 7.3 %synthesise_y.6.refs_0_ = f32[24,256,1024]{2,1,0:T(8,128)} custom-call(f32[8,4,64,256]{3,2,1,0:T(8,128)} %copy-done, bf16[512,1024]{1,0:T(8,128)(2,1)} %get-tuple-element.14.bh, bf16[512,1024]{1,0:T(8,128)(2,1)} %get-tuple-element.13.bl), custom_call_target="tpu_custom_call" | custom-call | flops 3221225472 | bytes 6291456 | tf_op jit(solution)/shard_map/synthesise_y/pallas_call | solution.py:188
  656.1 7.3 %synthesise_y.7.refs_0_ = f32[24,256,1024]{2,1,0:T(8,128)} custom-call(f32[8,4,64,256]{3,2,1,0:T(8,128)} %copy-done.2, bf16[512,1024]{1,0:T(8,128)(2,1)} %get-tuple-element.14.bh, bf16[512,1024]{1,0:T(8,128)(2,1)} %get-tuple-element.13.bl, f32[24,256,1024]{2,1,0:T(8,128)} %synthesise_y.6.refs_0_), custom_call_target="tpu_custom_call", output_to_operand_aliasing={{}: (3, {})} | custom-call | flops 3221225472 | bytes 6291456 | tf_op jit(solution)/shard_map/synthesise_y/pallas_call | solution.py:188
  663.3 7.2 %synthesise_y.8.refs_0_ = f32[24,256,1024]{2,1,0:T(8,128)} custom-call(f32[8,4,64,256]{3,2,1,0:T(8,128)} %all-to-all-done.7.coeffs, bf16[512,1024]{1,0:T(8,128)(2,1)} %get-tuple-element.14.bh, bf16[512,1024]{1,0:T(8,128)(2,1)} %get-tuple-element.13.bl, f32[24,256,1024]{2,1,0:T(8,128)} %synthesise_y.7.refs_0_), custom_call_target="tpu_custom_call", output_to_operand_aliasing={{}: (3, {})} | custom-call | flops 3221225472 | bytes 6291456 | tf_op jit(solution)/shard_map/synthesise_y/pallas_call | solution.py:188
  670.6 7.2 %synthesise_y.9.refs_0_ = f32[24,256,1024]{2,1,0:T(8,128)} custom-call(f32[8,4,64,256]{3,2,1,0:T(8,128)} %copy-done.1, bf16[512,1024]{1,0:T(8,128)(2,1)} %get-tuple-element.14.bh, bf16[512,1024]{1,0:T(8,128)(2,1)} %get-tuple-element.13.bl, f32[24,256,1024]{2,1,0:T(8,128)} %synthesise_y.8.refs_0_), custom_call_target="tpu_custom_call", output_to_operand_aliasing={{}: (3, {})} | custom-call | flops 3221225472 | bytes 6291456 | tf_op jit(solution)/shard_map/synthesise_y/pallas_call | solution.py:188
  677.8 7.2 %synthesise_y.10.refs_0_ = f32[24,256,1024]{2,1,0:T(8,128)} custom-call(f32[8,4,64,256]{3,2,1,0:T(8,128)} %all-to-all-done.3.coeffs, bf16[512,1024]{1,0:T(8,128)(2,1)} %get-tuple-element.14.bh, bf16[512,1024]{1,0:T(8,128)(2,1)} %get-tuple-element.13.bl, f32[24,256,1024]{2,1,0:T(8,128)} %synthesise_y.9.refs_0_), custom_call_target="tpu_custom_call", output_to_operand_aliasing={{}: (3, {})} | custom-call | flops 3221225472 | bytes 6291456 | tf_op jit(solution)/shard_map/synthesise_y/pallas_call | solution.py:188
  685.1 12.7 %all-to-all-done.1.coeffs = f32[8,4,64,256]{3,2,1,0:T(8,128)} async-done(((f32[8,4,64,256]{3,2,1,0:T(8,128)}), f32[8,4,64,256]{3,2,1,0:T(8,128)}, u32[]{:S(2)}, u32[]{:S(2)}) %all-to-all-start.1) | async-done | bytes 2097184 | tf_op jit(solution)/shard_map/all_to_all | solution.py:182
  697.8 7.3 %synthesise_y.11 = f32[24,256,1024]{2,1,0:T(8,128)} custom-call(f32[8,4,64,256]{3,2,1,0:T(8,128)} %all-to-all-done.1.coeffs, bf16[512,1024]{1,0:T(8,128)(2,1)} %get-tuple-element.14.bh, bf16[512,1024]{1,0:T(8,128)(2,1)} %get-tuple-element.13.bl, f32[24,256,1024]{2,1,0:T(8,128)} %synthesise_y.10.refs_0_), custom_call_target="tpu_custom_call", output_to_operand_aliasing={{}: (3, {})} | custom-call | flops 3221225472 | bytes 6291456 | tf_op jit(solution)/shard_map/synthesise_y/pallas_call | solution.py:188
  (74 shorter events, 49.1 us)
Async XLA Ops:
  13.1 55.4 %all-to-all-start.10 = ((f32[8,4,64,256]{3,2,1,0:T(8,128)}), f32[8,4,64,256]{3,2,1,0:T(8,128)S(1)}, u32[]{:S(2)}, u32[]{:S(2)}) async-start(f32[8,4,64,256]{3,2,1,0:T(8,128)} %analyse_y.11), calls=%async_computation.10 | async-start | bytes 4194304 | tf_op jit(solution)/shard_map/all_to_all | solution.py:143
  68.5 11.7 %copy-start.3 = (f32[8,4,64,256]{3,2,1,0:T(8,128)}, f32[8,4,64,256]{3,2,1,0:T(8,128)S(1)}, u32[]{:S(2)}) copy-start(f32[8,4,64,256]{3,2,1,0:T(8,128)S(1)} %all-to-all-done.10.lines) | copy-start | bytes 6291460
  68.5 53.4 %all-to-all-start.8 = ((f32[8,4,64,256]{3,2,1,0:T(8,128)}), f32[8,4,64,256]{3,2,1,0:T(8,128)}, u32[]{:S(2)}, u32[]{:S(2)}) async-start(f32[8,4,64,256]{3,2,1,0:T(8,128)} %analyse_y.10), calls=%async_computation.8 | async-start | bytes 4194304 | tf_op jit(solution)/shard_map/all_to_all | solution.py:143
  121.9 52.6 %all-to-all-start.6 = ((f32[8,4,64,256]{3,2,1,0:T(8,128)}), f32[8,4,64,256]{3,2,1,0:T(8,128)S(1)}, u32[]{:S(2)}, u32[]{:S(2)}) async-start(f32[8,4,64,256]{3,2,1,0:T(8,128)} %analyse_y.9), calls=%async_computation.6 | async-start | bytes 4194304 | tf_op jit(solution)/shard_map/all_to_all | solution.py:143
  174.5 11.7 %copy-start.4 = (f32[8,4,64,256]{3,2,1,0:T(8,128)}, f32[8,4,64,256]{3,2,1,0:T(8,128)S(1)}, u32[]{:S(2)}) copy-start(f32[8,4,64,256]{3,2,1,0:T(8,128)S(1)} %all-to-all-done.6.lines) | copy-start | bytes 6291460
  174.5 53.4 %all-to-all-start.4 = ((f32[8,4,64,256]{3,2,1,0:T(8,128)}), f32[8,4,64,256]{3,2,1,0:T(8,128)}, u32[]{:S(2)}, u32[]{:S(2)}) async-start(f32[8,4,64,256]{3,2,1,0:T(8,128)} %analyse_y.8), calls=%async_computation.4 | async-start | bytes 4194304 | tf_op jit(solution)/shard_map/all_to_all | solution.py:143
  186.2 46.9 %copy-start.9 = (s32[1,2,8]{2,1,0:T(2,128)S(1)}, s32[1,2,8]{2,1,0:T(2,128)}, u32[]{:S(2)}) copy-start(s32[1,2,8]{2,1,0:T(2,128)} %param.5) | copy-start | bytes 196
  227.9 52.6 %all-to-all-start.2 = ((f32[8,4,64,256]{3,2,1,0:T(8,128)}), f32[8,4,64,256]{3,2,1,0:T(8,128)S(1)}, u32[]{:S(2)}, u32[]{:S(2)}) async-start(f32[8,4,64,256]{3,2,1,0:T(8,128)} %analyse_y.7), calls=%async_computation.2 | async-start | bytes 4194304 | tf_op jit(solution)/shard_map/all_to_all | solution.py:143
  280.5 26.4 %copy-start.5 = (f32[8,4,64,256]{3,2,1,0:T(8,128)}, f32[8,4,64,256]{3,2,1,0:T(8,128)S(1)}, u32[]{:S(2)}) copy-start(f32[8,4,64,256]{3,2,1,0:T(8,128)S(1)} %all-to-all-done.2.lines) | copy-start | bytes 6291460
  280.5 71.9 %all-to-all-start = ((f32[8,4,64,256]{3,2,1,0:T(8,128)}), f32[8,4,64,256]{3,2,1,0:T(8,128)}, u32[]{:S(2)}, u32[]{:S(2)}) async-start(f32[8,4,64,256]{3,2,1,0:T(8,128)} %analyse_y.6), calls=%async_computation | async-start | bytes 4194304 | tf_op jit(solution)/shard_map/all_to_all | solution.py:143
  352.4 8.4 %copy-start.6 = (f32[4,64,1024]{2,1,0:T(8,128)S(1)}, f32[4,64,1024]{2,1,0:T(8,128)}, u32[]{:S(2)}) copy-start(f32[4,64,1024]{2,1,0:T(8,128)} %analyse_x.10.spectra) | copy-start | bytes 3145732
  352.4 8.4 %copy-start.7 = (f32[4,64,1024]{2,1,0:T(8,128)S(1)}, f32[4,64,1024]{2,1,0:T(8,128)}, u32[]{:S(2)}) copy-start(f32[4,64,1024]{2,1,0:T(8,128)} %analyse_x.9.spectra) | copy-start | bytes 3145732
  352.4 8.4 %copy-start.8 = (f32[4,64,1024]{2,1,0:T(8,128)S(1)}, f32[4,64,1024]{2,1,0:T(8,128)}, u32[]{:S(2)}) copy-start(f32[4,64,1024]{2,1,0:T(8,128)} %analyse_x.8.spectra) | copy-start | bytes 3145732
  363.1 4.5 collective-permute-start.5
  378.1 54.1 %all-to-all-start.11 = ((f32[8,4,64,256]{3,2,1,0:T(8,128)}), f32[8,4,64,256]{3,2,1,0:T(8,128)S(1)}, u32[]{:S(2)}, u32[]{:S(2)}) async-start(f32[8,4,64,256]{3,2,1,0:T(8,128)} %synthesise_x.11), calls=%async_computation.11 | async-start | bytes 4194304 | tf_op jit(solution)/shard_map/all_to_all | solution.py:182
  383.2 4.5 collective-permute-start.1
  432.2 19.4 %copy-start = (f32[8,4,64,256]{3,2,1,0:T(8,128)}, f32[8,4,64,256]{3,2,1,0:T(8,128)S(1)}, u32[]{:S(2)}) copy-start(f32[8,4,64,256]{3,2,1,0:T(8,128)S(1)} %all-to-all-done.11.coeffs) | copy-start | bytes 6291460
  432.2 53.4 %all-to-all-start.3 = ((f32[8,4,64,256]{3,2,1,0:T(8,128)}), f32[8,4,64,256]{3,2,1,0:T(8,128)}, u32[]{:S(2)}, u32[]{:S(2)}) async-start(f32[8,4,64,256]{3,2,1,0:T(8,128)} %synthesise_x.7), calls=%async_computation.3 | async-start | bytes 4194304 | tf_op jit(solution)/shard_map/all_to_all | solution.py:182
  436.6 4.5 collective-permute-start.2
  485.6 52.6 %all-to-all-start.5 = ((f32[8,4,64,256]{3,2,1,0:T(8,128)}), f32[8,4,64,256]{3,2,1,0:T(8,128)S(1)}, u32[]{:S(2)}, u32[]{:S(2)}) async-start(f32[8,4,64,256]{3,2,1,0:T(8,128)} %synthesise_x.8), calls=%async_computation.5 | async-start | bytes 4194304 | tf_op jit(solution)/shard_map/all_to_all | solution.py:182
  489.3 4.5 collective-permute-start.3
  538.2 19.4 %copy-start.1 = (f32[8,4,64,256]{3,2,1,0:T(8,128)}, f32[8,4,64,256]{3,2,1,0:T(8,128)S(1)}, u32[]{:S(2)}) copy-start(f32[8,4,64,256]{3,2,1,0:T(8,128)S(1)} %all-to-all-done.5.coeffs) | copy-start | bytes 6291460
  538.2 53.4 %all-to-all-start.7 = ((f32[8,4,64,256]{3,2,1,0:T(8,128)}), f32[8,4,64,256]{3,2,1,0:T(8,128)}, u32[]{:S(2)}, u32[]{:S(2)}) async-start(f32[8,4,64,256]{3,2,1,0:T(8,128)} %synthesise_x.9), calls=%async_computation.7 | async-start | bytes 4194304 | tf_op jit(solution)/shard_map/all_to_all | solution.py:182
  542.6 4.5 collective-permute-start.4
  591.6 52.6 %all-to-all-start.9 = ((f32[8,4,64,256]{3,2,1,0:T(8,128)}), f32[8,4,64,256]{3,2,1,0:T(8,128)S(1)}, u32[]{:S(2)}, u32[]{:S(2)}) async-start(f32[8,4,64,256]{3,2,1,0:T(8,128)} %synthesise_x.10), calls=%async_computation.9 | async-start | bytes 4194304 | tf_op jit(solution)/shard_map/all_to_all | solution.py:182
  595.2 4.5 collective-permute-start
  644.2 11.9 %copy-start.2 = (f32[8,4,64,256]{3,2,1,0:T(8,128)}, f32[8,4,64,256]{3,2,1,0:T(8,128)S(1)}, u32[]{:S(2)}) copy-start(f32[8,4,64,256]{3,2,1,0:T(8,128)S(1)} %all-to-all-done.9.coeffs) | copy-start | bytes 6291460
  644.2 53.6 %all-to-all-start.1 = ((f32[8,4,64,256]{3,2,1,0:T(8,128)}), f32[8,4,64,256]{3,2,1,0:T(8,128)}, u32[]{:S(2)}, u32[]{:S(2)}) async-start(f32[8,4,64,256]{3,2,1,0:T(8,128)} %synthesise_x.6), calls=%async_computation.1 | async-start | bytes 4194304 | tf_op jit(solution)/shard_map/all_to_all | solution.py:182
